TPU v7x, 32 devices: a whole 2x2x4 slice. The times are simulated.
32 devices in a mesh: groups: 2 (over y), wide: 8 (over z, x), narrow: 2 (over core).
Axes of the slice: x: 2, y: 2, z: 4, core: 2. Of those that a mesh axis runs over, the one named last changes fastest.
Arguments:
- hidden_in: bfloat16 [6400, 1024], P(('groups', 'wide')), parts along dimension 0, may hold values from -6 to 6
- ffn_gain: bfloat16 [1024], replicated, may hold values from 0.5 to 1.5
- wi_gate: bfloat16 [1024, 2816], P('wide', 'narrow'), may hold values from -0.1875 to 0.1875
- wi_up: bfloat16 [1024, 2816], P('wide', 'narrow'), may hold values from -0.1875 to 0.1875
- wo_down: bfloat16 [2816, 1024], P('narrow', 'wide'), may hold values from -0.109375 to 0.109375
- final_gain: bfloat16 [1024], replicated, may hold values from 0.5 to 1.5
- key_w: bfloat16 [1024, 1024], P('wide', 'narrow'), may hold values from -0.1875 to 0.1875
- value_w: bfloat16 [1024, 1024], P('wide', 'narrow'), may hold values from -0.1875 to 0.1875
- query_w: bfloat16 [1024, 1024], P('wide', 'narrow'), may hold values from -8 to 8
- out_w: bfloat16 [1024, 1024], P('narrow', 'wide'), may hold values from -0.1875 to 0.1875
- dec_gain: bfloat16 [1024], replicated, may hold values from 0.5 to 1.5
- embed: bfloat16 [32128, 1024], P('wide'), may hold values from -6 to 6
- lengths: int32 [32], P(('groups', 'wide')), parts along dimension 0, may hold values from 40 to 200
- answer_ids: int32 [8, 32], P('groups'), parts along dimension 0, may hold values from 0 to 32127
Outputs:
- memory: bfloat16 [6400, 1024], P(('groups', 'wide')), parts along dimension 0
- decoded: bfloat16 [256, 1024], P('groups', 'narrow'), parts along dimension 0
There are 2 independent parts, one for each index of `groups`. A program takes and returns all parts, laid end to end along the dimension named above; an argument that names none is the same for every part. Nothing has to cross between parts.
All inputs are finite; a program needn't handle non-finite values.
Results may differ from a plain program's by a relative error of at most 0.0095.
The roundings to bfloat16 on the way count: a program that leaves them out, or rounds other values in their place, can miss the bound.
Values may be sent and summed in bfloat16 or wider, within the bound.
A program may use at most 64 MiB of HBM per device.

v0:
```python
import math
import jax
import jax.numpy as jnp
from jax import lax
from jax.sharding import PartitionSpec as P

HEAD_DIM = 64
QUEST = 4
EPS = 1e-06
FLOOR = -1e30


def joined(part, axis, combine):
    gathered = jax.tree.map(lambda a: lax.all_gather(a, axis), part)

    def take(source):
        return jax.tree.map(lambda a: lax.dynamic_index_in_dim(a, source, 0, False), gathered)

    return lax.fori_loop(
        1, lax.axis_size(axis), lambda source, state: combine(state, take(source)), take(0)
    )


def rms_scale(values, gain):
    mean_square = jnp.mean(values * values, axis=-1, keepdims=True)
    return values * lax.rsqrt(mean_square + EPS) * gain.astype(jnp.float32)


def add_rows(left, piece):
    return jnp.dot(left, piece, preferred_element_type=jnp.float32)


def join_partial(first, second):
    top_first, total_first, acc_first = first
    top_second, total_second, acc_second = second
    top = jnp.maximum(top_first, top_second)
    factor_first = jnp.exp(top_first - top)
    factor_second = jnp.exp(top_second - top)
    width = acc_first.shape[1] // top.shape[1]
    total = total_first * factor_first + total_second * factor_second
    acc = acc_first * jnp.repeat(factor_first, width, axis=1) + acc_second * jnp.repeat(
        factor_second, width, axis=1
    )
    return (top, total, acc)


def per_device(
    hidden_in,
    ffn_gain,
    wi_gate,
    wi_up,
    wo_down,
    final_gain,
    key_w,
    value_w,
    query_w,
    out_w,
    dec_gain,
    embed,
    lengths,
    answer_ids,
):
    rows = hidden_in.shape[0]
    features = hidden_in.shape[1]
    resid_in = hidden_in.astype(jnp.float32)
    enc_in = rms_scale(resid_in, ffn_gain).astype(jnp.bfloat16)

    def add_one(piece):
        return add_rows(enc_in, piece)

    gate = add_one(lax.all_gather(wi_gate, "wide", axis=0, tiled=True))
    up = add_one(lax.all_gather(wi_up, "wide", axis=0, tiled=True))
    inner = (jax.nn.gelu(gate, approximate=True) * up).astype(jnp.bfloat16)
    partial_down = jnp.dot(
        inner,
        lax.all_gather(wo_down, "wide", axis=1, tiled=True),
        preferred_element_type=jnp.float32,
    )
    share = lax.psum_scatter(partial_down, "narrow", scatter_dimension=1, tiled=True)
    half = share.shape[1]
    offset = lax.axis_index("narrow") * half
    resid_half = lax.dynamic_slice_in_dim(resid_in, offset, half, 1) + share
    squares = lax.psum(jnp.sum(resid_half * resid_half, axis=1, keepdims=True), "narrow")
    gain_half = lax.dynamic_slice_in_dim(final_gain, offset, half, 0).astype(jnp.float32)
    memory_half = (resid_half * lax.rsqrt(squares / features + EPS) * gain_half).astype(
        jnp.bfloat16
    )
    memory = lax.all_gather(memory_half, "narrow", axis=1, tiled=True)
    pass_dev = lengths.shape[0]
    per_question = pass_dev * lax.axis_size("wide") // QUEST
    question = lax.axis_index("wide") * pass_dev // per_question
    answers = answer_ids.shape[1]
    qrows = answer_ids.shape[0] * answers
    vocab_rows = embed.shape[0]
    local_ids = answer_ids.reshape(qrows) - lax.axis_index("wide") * vocab_rows
    onehot = (local_ids[:, None] == jnp.arange(vocab_rows, dtype=jnp.int32)[None, :]).astype(
        jnp.bfloat16
    )
    embedded = lax.psum(jnp.dot(onehot, embed, preferred_element_type=jnp.float32), "wide")
    dec_in = rms_scale(embedded, dec_gain).astype(jnp.bfloat16)
    own_rows = lax.dynamic_slice_in_dim(dec_in, question * answers, answers, 0)
    proj_cols = key_w.shape[1]
    keys_sum = add_rows(memory, lax.all_gather(key_w, "wide", axis=0, tiled=True))
    values_sum = add_rows(memory, lax.all_gather(value_w, "wide", axis=0, tiled=True))
    query_sum = add_rows(own_rows, lax.all_gather(query_w, "wide", axis=0, tiled=True))
    keys = keys_sum.astype(jnp.bfloat16)
    values = values_sum.astype(jnp.bfloat16)
    query = query_sum.astype(jnp.bfloat16)
    heads_local = proj_cols // HEAD_DIM
    query_three = query.reshape(answers, heads_local, HEAD_DIM)
    keys_three = keys.reshape(rows, heads_local, HEAD_DIM)
    values_three = values.reshape(rows, heads_local, HEAD_DIM).astype(jnp.float32)
    scores = jnp.einsum(
        "ahd,khd->ahk", query_three, keys_three, preferred_element_type=jnp.float32
    ) * (1.0 / math.sqrt(HEAD_DIM))
    passage_len = rows // pass_dev
    live = (jnp.arange(passage_len, dtype=jnp.int32)[None, :] < lengths[:, None]).reshape(rows)
    scores = jnp.where(live[None, None, :], scores, FLOOR)
    top = jnp.max(scores, axis=2)
    weights = jnp.exp(scores - top[:, :, None])
    total = jnp.sum(weights, axis=2)
    acc = jnp.einsum(
        "ahk,khd->ahd", weights, values_three, precision=lax.Precision.HIGHEST
    ).reshape(answers, proj_cols)
    start_row = question * answers
    top_all = lax.dynamic_update_slice_in_dim(
        jnp.full((qrows, heads_local), FLOOR, jnp.float32), top, start_row, 0
    )
    total_all = lax.dynamic_update_slice_in_dim(
        jnp.zeros((qrows, heads_local), jnp.float32), total, start_row, 0
    )
    acc_all = lax.dynamic_update_slice_in_dim(
        jnp.zeros((qrows, proj_cols), jnp.float32), acc, start_row, 0
    )
    top_all, total_all, acc_all = joined((top_all, total_all, acc_all), "wide", join_partial)
    attended = (acc_all / jnp.repeat(total_all, HEAD_DIM, axis=1)).astype(jnp.bfloat16)
    partial_out = jnp.dot(
        attended,
        lax.all_gather(out_w, "wide", axis=1, tiled=True),
        preferred_element_type=jnp.float32,
    )
    share_out = lax.psum_scatter(
        partial_out.astype(jnp.bfloat16), "narrow", scatter_dimension=1, tiled=True
    ).astype(jnp.float32)
    out_half = share_out.shape[1]
    embedded_half = lax.dynamic_slice_in_dim(
        embedded, lax.axis_index("narrow") * out_half, out_half, 1
    )
    decoded = (embedded_half + share_out).astype(jnp.bfloat16)
    return (memory, decoded)


def solution(mesh):
    placed = (
        P(("groups", "wide"), None),
        P(),
        P("wide", "narrow"),
        P("wide", "narrow"),
        P("narrow", "wide"),
        P(),
        P("wide", "narrow"),
        P("wide", "narrow"),
        P("wide", "narrow"),
        P("narrow", "wide"),
        P(),
        P("wide", None),
        P(("groups", "wide")),
        P("groups", None),
    )
    return jax.shard_map(
        per_device,
        mesh=mesh,
        in_specs=placed,
        out_specs=(P(("groups", "wide"), None), P("groups", "narrow")),
        check_vma=False,
    )
```

profile of v0, /device:TPU:0, one launch (start us, length us, event | category | flops | bytes accessed | tf_op | source)
XLA Modules:
  0.0 510.4 jit_solution(5769882947036449101)
XLA Ops:
  10.2 5.5 %fusion.11 = f32[128,1024]{1,0:T(8,128)} fusion(bf16[4016,1024]{1,0:T(8,128)(2,1)} %param.27, s32[128]{0:T(128)S(1)} %sub.47), kind=kOutput, calls=%fused_computation.21 | convolution fusion | flops 1053284352 | bytes 8749568 | tf_op jit(solution)/shard_map/dot_general | solution.py:99
  16.7 53.5 %all-gather.9.cloned.1.call-done = bf16[1024,1408]{1,0:T(8,128)(2,1)} async-done(((bf16[128,1408]{1,0:T(8,128)(2,1)}), bf16[1024,1408]{1,0:T(8,128)(2,1)}) %all-gather.9.cloned.1.call-update) | async-done | bytes 2883600 | tf_op jit(solution)/shard_map/all_gather | solution.py:71
  70.2 3.3 fusion.19
  73.5 54.8 %all-gather.11.cloned.1.call-done = bf16[1024,1408]{1,0:T(8,128)(2,1)} async-done(((bf16[128,1408]{1,0:T(8,128)(2,1)}), bf16[1024,1408]{1,0:T(8,128)(2,1)}) %all-gather.11.cloned.1.call-update) | async-done | bytes 2883600 | tf_op jit(solution)/shard_map/all_gather | solution.py:72
  128.3 60.3 %all-gather.13.cloned.1.call-done = bf16[1408,1024]{1,0:T(8,128)(2,1)} async-done(((bf16[1408,128]{1,0:T(8,128)(2,1)}), bf16[1408,1024]{1,0:T(8,128)(2,1)}) %all-gather.13.cloned.1.call-update) | async-done | bytes 2883600 | tf_op jit(solution)/shard_map/all_gather | solution.py:76
  188.6 6.7 %fusion.15 = f32[400,1024]{1,0:T(8,128)} fusion(bf16[1408,1024]{1,0:T(8,128)(2,1)} %all-gather.13.cloned.1.call-done, bf16[1024,1408]{1,0:T(8,128)(2,1)} %all-gather.11.cloned.1.call-done, f32[400,1408]{1,0:T(8,128)S(1)} %fusion.19, f32[1024]{0:T(1024)S(1)} %convert_element_type.48, f32[400]{0:T(512)S(1)} %add_rsqrt_fusion.1, bf16[400,1024]{1,0:T(8,128)(2,1)S(1)} %copy-done), kind=kOutput, calls=%fused_computation.36 | convolution fusion | flops 2314137600 | bytes 10483264 | tf_op jit(solution)/shard_map/dot_general | solution.py:74
  197.4 65.9 %all-reduce.2.cloned.1.call-done = f32[128,1024]{1,0:T(8,128)} async-done(((f32[128,1024]{1,0:T(8,128)}), f32[128,1024]{1,0:T(8,128)}) %all-reduce.2.cloned.1.call-update) | async-done | bytes 524304 | tf_op jit(solution)/shard_map/psum | solution.py:99
  264.5 40.2 %all-gather.17.cloned.1.call-done = bf16[1024,512]{1,0:T(8,128)(2,1)} async-done(((bf16[128,512]{1,0:T(8,128)(2,1)}), bf16[1024,512]{1,0:T(8,128)(2,1)}) %all-gather.17.cloned.1.call-update) | async-done | bytes 1048592 | tf_op jit(solution)/shard_map/all_gather | solution.py:105
  304.7 1.6 convolution_convert_fusion.3
  306.5 8.1 %reduce-scatter.3.cloned.1.call-done = f32[400,512]{1,0:T(8,128)} async-done(((f32[400,1024]{1,0:T(8,128)}), f32[400,512]{1,0:T(8,128)}) %reduce-scatter.3.cloned.1.call-update) | async-done | bytes 819216 | tf_op jit(solution)/shard_map/reduce_scatter | solution.py:79
  314.6 1.3 multiply_reduce_fusion.1
  315.9 2.5 psum.14
  319.7 2.4 all_gather.45
  322.1 36.2 %all-gather.15.cloned.1.call-done = bf16[1024,512]{1,0:T(8,128)(2,1)} async-done(((bf16[128,512]{1,0:T(8,128)(2,1)}), bf16[1024,512]{1,0:T(8,128)(2,1)}) %all-gather.15.cloned.1.call-update) | async-done | bytes 1048592 | tf_op jit(solution)/shard_map/all_gather | solution.py:103
  358.3 1.8 convolution_convert_fusion.1
  360.3 39.1 %all-gather.19.cloned.1.call-done = bf16[1024,512]{1,0:T(8,128)(2,1)} async-done(((bf16[128,512]{1,0:T(8,128)(2,1)}), bf16[1024,512]{1,0:T(8,128)(2,1)}) %all-gather.19.cloned.1.call-update) | async-done | bytes 1048592 | tf_op jit(solution)/shard_map/all_gather | solution.py:104
  399.5 1.8 convolution_convert_fusion
  404.4 30.8 %all_gather.51 = f32[8,128,8]{1,2,0:T(8,128)S(1)} all-gather(f32[1,128,8]{1,2,0:T(8,128)S(1)} %dynamic_update_slice.13), channel_id=1, replica_groups=mesh['groups'=2,'wide'=8,'narrow'=2] {'wide'}, dimensions={0}, use_global_device_ids=true | all-gather | bytes 36864 | tf_op jit(solution)/shard_map/all_gather | solution.py:14
  435.4 31.0 %all_gather.49 = f32[8,128,8]{1,2,0:T(8,128)S(1)} all-gather(f32[1,128,8]{1,2,0:T(8,128)S(1)} %dynamic_update_slice.12), channel_id=1, replica_groups=mesh['groups'=2,'wide'=8,'narrow'=2] {'wide'}, dimensions={0}, use_global_device_ids=true | all-gather | bytes 36864 | tf_op jit(solution)/shard_map/all_gather | solution.py:14
  467.5 8.8 %while.19 = (s32[]{:T(128)}, f32[128,8]{0,1:T(8,128)S(1)}, f32[128,8]{0,1:T(8,128)S(1)}, f32[128,512]{0,1:T(8,128)S(1)}, f32[8,128,8]{1,2,0:T(8,128)S(1)}, /*ind...) while((s32[]{:T(128)}, f32[128,8]{0,1:T(8,128)S(1)}, ...), condition=%wide.region_9.10_spmd, body=%wide.region_8.9_spmd.sunk | while | flops 202757 | bytes 1876119 | solution.py:19
  476.3 15.4 %all-gather.23.cloned.1.call-done = bf16[512,1024]{1,0:T(8,128)(2,1)} async-done(((bf16[512,128]{1,0:T(8,128)(2,1)}), bf16[512,1024]{1,0:T(8,128)(2,1)}) %all-gather.23.cloned.1.call-update) | async-done | bytes 1048592 | tf_op jit(solution)/shard_map/all_gather | solution.py:139
  491.8 2.3 convolution_convert_fusion.2
  494.0 7.3 %reduce-scatter.5.cloned.1.call-done = bf16[128,512]{1,0:T(8,128)(2,1)} async-done(((bf16[128,1024]{1,0:T(8,128)(2,1)}), bf16[128,512]{1,0:T(8,128)(2,1)}) %reduce-scatter.5.cloned.1.call-update) | async-done | bytes 131088 | tf_op jit(solution)/shard_map/reduce_scatter | solution.py:142
  501.4 1.6 add_convert_fusion
  (100 shorter events, 22.5 us)
Async XLA Ops:
  7.2 63.0 %all-gather.9.cloned.1.call-start = ((), (), s32[]{:S(2)}) async-start(), calls=%async_computation.2 | async-start | bytes 3244032 | tf_op jit(solution)/shard_map/all_gather | solution.py:71
  7.9 120.4 %all-gather.11.cloned.1.call-start = ((), (), s32[]{:S(2)}) async-start(), calls=%async_computation.3 | async-start | bytes 3244032 | tf_op jit(solution)/shard_map/all_gather | solution.py:72
  8.6 180.0 %all-gather.13.cloned.1.call-start = ((), (), s32[]{:S(2)}) async-start(), calls=%async_computation.4 | async-start | bytes 3244032 | tf_op jit(solution)/shard_map/all_gather | solution.py:76
  9.4 253.9 %all-reduce.2.cloned.1.call-start = ((), (), s32[]{:S(2)}) async-start(), calls=%async_computation.6 | async-start | bytes 1048576 | tf_op jit(solution)/shard_map/psum | solution.py:99
  10.2 6.2 %copy-start.3 = (bf16[1024]{0:T(1024)(128)(2,1)S(1)}, bf16[1024]{0:T(1024)(128)(2,1)}, u32[]{:S(2)}) copy-start(bf16[1024]{0:T(1024)(128)(2,1)} %param.17) | copy-start | bytes 6148
  10.2 6.2 %copy-start = (bf16[400,1024]{1,0:T(8,128)(2,1)S(1)}, bf16[400,1024]{1,0:T(8,128)(2,1)}, u32[]{:S(2)}) copy-start(bf16[400,1024]{1,0:T(8,128)(2,1)} %param.16) | copy-start | bytes 2457604
  15.7 289.0 %all-gather.17.cloned.1.call-start = ((), (), s32[]{:S(2)}) async-start(), calls=%async_computation.8 | async-start | bytes 1179648 | tf_op jit(solution)/shard_map/all_gather | solution.py:105
  16.3 298.3 %reduce-scatter.3.cloned.1.call-start = ((), (), s32[]{:S(2)}) async-start(), calls=%async_computation.5 | async-start | bytes 2457600 | tf_op jit(solution)/shard_map/reduce_scatter | solution.py:79
  195.3 1.8 copy-start.4
  195.3 1.8 copy-start.6
  195.3 2.0 copy-start.5
  195.4 162.9 %all-gather.15.cloned.1.call-start = ((), (), s32[]{:S(2)}) async-start(), calls=%async_computation.7 | async-start | bytes 1179648 | tf_op jit(solution)/shard_map/all_gather | solution.py:103
  196.1 203.3 %all-gather.19.cloned.1.call-start = ((), (), s32[]{:S(2)}) async-start(), calls=%async_computation.9 | async-start | bytes 1179648 | tf_op jit(solution)/shard_map/all_gather | solution.py:104
  196.9 269.5 %all-gather.21.cloned.1.call-start = ((), (), s32[]{:S(2)}) async-start(), calls=%async_computation.10 | async-start | bytes 2359296 | tf_op jit(solution)/shard_map/all_gather | solution.py:14
  402.6 0.7 copy-start.2
  403.3 88.4 %all-gather.23.cloned.1.call-start = ((), (), s32[]{:S(2)}) async-start(), calls=%async_computation.11 | async-start | bytes 1179648 | tf_op jit(solution)/shard_map/all_gather | solution.py:139
  403.9 97.4 %reduce-scatter.5.cloned.1.call-start = ((), (), s32[]{:S(2)}) async-start(), calls=%async_computation.12 | async-start | bytes 393216 | tf_op jit(solution)/shard_map/reduce_scatter | solution.py:142
  476.3 25.1 %copy-start.1 = (f32[128,1024]{1,0:T(8,128)S(1)}, f32[128,1024]{1,0:T(8,128)}, u32[]{:S(2)}) copy-start(f32[128,1024]{1,0:T(8,128)} %all-reduce.2.cloned.1.call-done) | copy-start | bytes 1572868
Sparse Core Ops, SparseCore 0:
  10.2 60.0 all-gather.8
  72.4 55.9 all-gather.10
  130.4 58.1 all-gather.12
  192.5 70.7 all-reduce.1
  265.2 39.4 all-gather.16
  306.8 7.7 reduce-scatter.2
  316.7 41.5 all-gather.14
  360.4 38.9 all-gather.18
  403.5 48.3 all-gather.20
  453.8 37.9 all-gather.22
  494.6 6.7 reduce-scatter.4
where the time goes:
time: 511 us; the launch traced here: 510 us
  waiting for transfers between devices  385 us (75%)
  blocking collectives  66.6 us (13%)
  matrix products  24 us (5%)
  between operations  14.1 us (3%)
  local copies, waits for them, and re-layouts  11.7 us (2%)
  other arithmetic  7.71 us (2%)
    psum x1, waiting for transfers between devices, per_device(): lax.psum(jnp.dot(onehot, embed, preferred_element_type=jnp.float32), 'wide')  65.9 us
    all_gather x2, blocking collectives, joined(): gathered = jax.tree.map(lambda a: lax.all_gather(a, axis), part)  61.8 us
    all_gather x1, waiting for transfers between devices, per_device(): lax.all_gather(wo_down, 'wide', axis=1, tiled=True)  60.3 us
    all_gather x1, waiting for transfers between devices, per_device(): up = add_one(lax.all_gather(wi_up, 'wide', axis=0, tiled=True))  54.8 us
    all_gather x1, waiting for transfers between devices, per_device(): gate = add_one(lax.all_gather(wi_gate, 'wide', axis=0, tiled=True))  53.5 us
    all_gather x1, waiting for transfers between devices, per_device(): lax.all_gather(query_w, 'wide', axis=0, tiled=True)  40.2 us
    all_gather x1, waiting for transfers between devices, per_device(): lax.all_gather(value_w, 'wide', axis=0, tiled=True)  39.1 us
    all_gather x1, waiting for transfers between devices, per_device(): lax.all_gather(key_w, 'wide', axis=0, tiled=True)  36.2 us
  transfers between devices with their start and end apart: 11, of which 10 were waited for; matrix products, arithmetic and copies ran while one was open for 7% of the time, Pallas kernels for 0%

commit v1 on v0

--- a/solution.py
+++ b/solution.py
@@ -96,7 +96,9 @@
     onehot = (local_ids[:, None] == jnp.arange(vocab_rows, dtype=jnp.int32)[None, :]).astype(
         jnp.bfloat16
     )
-    embedded = lax.psum(jnp.dot(onehot, embed, preferred_element_type=jnp.float32), "wide")
+    embedded = jnp.sum(
+        lax.all_gather(jnp.dot(onehot, embed, preferred_element_type=jnp.float32), "wide"), axis=0
+    )
     dec_in = rms_scale(embedded, dec_gain).astype(jnp.bfloat16)
     own_rows = lax.dynamic_slice_in_dim(dec_in, question * answers, answers, 0)
     proj_cols = key_w.shape[1]

time: 511 us -> 509 us (level)
    psum x1 -> x0, waiting for transfers between devices: 65.9 us -> none  [per_device(): lax.psum(jnp.dot(onehot, embed, preferred_element_type=jnp.float32), 'wide')]
    all_gather x0 -> x1, waiting for transfers between devices: none -> 64.8 us  [per_device(): lax.all_gather(jnp.dot(onehot, embed, preferred_element_type=jnp.float32)...]
where the time goes in v1:
time: 509 us
  waiting for transfers between devices  382 us (75%)
  blocking collectives  66.7 us (13%)
  matrix products  23.8 us (5%)
  between operations  14.1 us (3%)
  local copies, waits for them, and re-layouts  11.7 us (2%)
  other arithmetic  9.3 us (2%)
    all_gather x1, waiting for transfers between devices, per_device(): lax.all_gather(jnp.dot(onehot, embed, preferred_element_type=jnp.float32)...  64.8 us
    all_gather x2, blocking collectives, joined(): gathered = jax.tree.map(lambda a: lax.all_gather(a, axis), part)  61.9 us
    all_gather x1, waiting for transfers between devices, per_device(): lax.all_gather(wo_down, 'wide', axis=1, tiled=True)  60.3 us
    all_gather x1, waiting for transfers between devices, per_device(): up = add_one(lax.all_gather(wi_up, 'wide', axis=0, tiled=True))  54.8 us
    all_gather x1, waiting for transfers between devices, per_device(): gate = add_one(lax.all_gather(wi_gate, 'wide', axis=0, tiled=True))  53.5 us
    all_gather x1, waiting for transfers between devices, per_device(): lax.all_gather(value_w, 'wide', axis=0, tiled=True)  39.1 us
    all_gather x1, waiting for transfers between devices, per_device(): lax.all_gather(query_w, 'wide', axis=0, tiled=True)  38 us
    all_gather x1, waiting for transfers between devices, per_device(): lax.all_gather(key_w, 'wide', axis=0, tiled=True)  36.2 us
  transfers between devices with their start and end apart: 11, of which 10 were waited for; matrix products, arithmetic and copies ran while one was open for 7% of the time, Pallas kernels for 0%

profile of v1, /device:TPU:0, one launch (start us, length us, event | category | flops | bytes accessed | tf_op | source)
XLA Modules:
  0.0 508.6 jit_solution(12754650451977029711)
XLA Ops:
  10.2 5.5 %fusion.11 = f32[128,1024]{1,0:T(8,128)} fusion(bf16[4016,1024]{1,0:T(8,128)(2,1)} %param.27, s32[128]{0:T(128)S(1)} %sub.47), kind=kOutput, calls=%fused_computation.21 | convolution fusion | flops 1053284352 | bytes 8749568 | tf_op jit(solution)/shard_map/dot_general | solution.py:100
  16.7 53.5 %all-gather.11.cloned.1.call-done = bf16[1024,1408]{1,0:T(8,128)(2,1)} async-done(((bf16[128,1408]{1,0:T(8,128)(2,1)}), bf16[1024,1408]{1,0:T(8,128)(2,1)}) %all-gather.11.cloned.1.call-update) | async-done | bytes 2883600 | tf_op jit(solution)/shard_map/all_gather | solution.py:71
  70.2 3.3 fusion.19
  73.5 54.8 %all-gather.13.cloned.1.call-done = bf16[1024,1408]{1,0:T(8,128)(2,1)} async-done(((bf16[128,1408]{1,0:T(8,128)(2,1)}), bf16[1024,1408]{1,0:T(8,128)(2,1)}) %all-gather.13.cloned.1.call-update) | async-done | bytes 2883600 | tf_op jit(solution)/shard_map/all_gather | solution.py:72
  128.3 60.3 %all-gather.15.cloned.1.call-done = bf16[1408,1024]{1,0:T(8,128)(2,1)} async-done(((bf16[1408,128]{1,0:T(8,128)(2,1)}), bf16[1408,1024]{1,0:T(8,128)(2,1)}) %all-gather.15.cloned.1.call-update) | async-done | bytes 2883600 | tf_op jit(solution)/shard_map/all_gather | solution.py:76
  188.6 6.7 %fusion.15 = f32[400,1024]{1,0:T(8,128)} fusion(bf16[1408,1024]{1,0:T(8,128)(2,1)} %all-gather.15.cloned.1.call-done, bf16[1024,1408]{1,0:T(8,128)(2,1)} %all-gather.13.cloned.1.call-done, f32[400,1408]{1,0:T(8,128)S(1)} %fusion.19, f32[1024]{0:T(1024)S(1)} %convert_element_type.48, f32[400]{0:T(512)S(1)} %add_rsqrt_fusion.1, bf16[400,1024]{1,0:T(8,128)(2,1)S(1)} %copy-done), kind=kOutput, calls=%fused_computation.36 | convolution fusion | flops 2314137600 | bytes 10483264 | tf_op jit(solution)/shard_map/dot_general | solution.py:74
  197.4 64.8 %all-gather.27.cloned.1.call-done = f32[1024,1024]{1,0:T(8,128)} async-done(((f32[128,1024]{1,0:T(8,128)}), f32[1024,1024]{1,0:T(8,128)}) %all-gather.27.cloned.1.call-update) | async-done | bytes 4194320 | tf_op jit(solution)/shard_map/all_gather | solution.py:100
  262.2 2.6 reduce_sum.47
  265.0 38.0 %all-gather.19.cloned.1.call-done = bf16[1024,512]{1,0:T(8,128)(2,1)} async-done(((bf16[128,512]{1,0:T(8,128)(2,1)}), bf16[1024,512]{1,0:T(8,128)(2,1)}) %all-gather.19.cloned.1.call-update) | async-done | bytes 1048592 | tf_op jit(solution)/shard_map/all_gather | solution.py:107
  303.0 1.5 convolution_convert_fusion.3
  304.6 8.2 %reduce-scatter.3.cloned.1.call-done = f32[400,512]{1,0:T(8,128)} async-done(((f32[400,1024]{1,0:T(8,128)}), f32[400,512]{1,0:T(8,128)}) %reduce-scatter.3.cloned.1.call-update) | async-done | bytes 819216 | tf_op jit(solution)/shard_map/reduce_scatter | solution.py:79
  314.2 2.5 psum.7
  318.0 2.4 all_gather.51
  320.3 36.2 %all-gather.17.cloned.1.call-done = bf16[1024,512]{1,0:T(8,128)(2,1)} async-done(((bf16[128,512]{1,0:T(8,128)(2,1)}), bf16[1024,512]{1,0:T(8,128)(2,1)}) %all-gather.17.cloned.1.call-update) | async-done | bytes 1048592 | tf_op jit(solution)/shard_map/all_gather | solution.py:105
  356.6 1.8 convolution_convert_fusion.1
  358.6 39.1 %all-gather.21.cloned.1.call-done = bf16[1024,512]{1,0:T(8,128)(2,1)} async-done(((bf16[128,512]{1,0:T(8,128)(2,1)}), bf16[1024,512]{1,0:T(8,128)(2,1)}) %all-gather.21.cloned.1.call-update) | async-done | bytes 1048592 | tf_op jit(solution)/shard_map/all_gather | solution.py:106
  397.7 1.8 convolution_convert_fusion
  402.7 30.8 %all_gather.59 = f32[8,128,8]{1,2,0:T(8,128)S(1)} all-gather(f32[1,128,8]{1,2,0:T(8,128)S(1)} %dynamic_update_slice.13), channel_id=1, replica_groups=mesh['groups'=2,'wide'=8,'narrow'=2] {'wide'}, dimensions={0}, use_global_device_ids=true | all-gather | bytes 36864 | tf_op jit(solution)/shard_map/all_gather | solution.py:14
  433.6 31.1 %all_gather.57 = f32[8,128,8]{1,2,0:T(8,128)S(1)} all-gather(f32[1,128,8]{1,2,0:T(8,128)S(1)} %dynamic_update_slice.12), channel_id=1, replica_groups=mesh['groups'=2,'wide'=8,'narrow'=2] {'wide'}, dimensions={0}, use_global_device_ids=true | all-gather | bytes 36864 | tf_op jit(solution)/shard_map/all_gather | solution.py:14
  465.8 8.8 %while.19 = (s32[]{:T(128)}, f32[128,8]{0,1:T(8,128)S(1)}, f32[128,8]{0,1:T(8,128)S(1)}, f32[128,512]{0,1:T(8,128)S(1)}, f32[8,128,8]{1,2,0:T(8,128)S(1)}, /*ind...) while((s32[]{:T(128)}, f32[128,8]{0,1:T(8,128)S(1)}, ...), condition=%wide.region_9.10_spmd, body=%wide.region_8.9_spmd.sunk | while | flops 202757 | bytes 1876119 | solution.py:19
  474.7 15.3 %all-gather.25.cloned.1.call-done = bf16[512,1024]{1,0:T(8,128)(2,1)} async-done(((bf16[512,128]{1,0:T(8,128)(2,1)}), bf16[512,1024]{1,0:T(8,128)(2,1)}) %all-gather.25.cloned.1.call-update) | async-done | bytes 1048592 | tf_op jit(solution)/shard_map/all_gather | solution.py:141
  490.0 2.3 convolution_convert_fusion.2
  492.3 7.3 %reduce-scatter.5.cloned.1.call-done = bf16[128,512]{1,0:T(8,128)(2,1)} async-done(((bf16[128,1024]{1,0:T(8,128)(2,1)}), bf16[128,512]{1,0:T(8,128)(2,1)}) %reduce-scatter.5.cloned.1.call-update) | async-done | bytes 131088 | tf_op jit(solution)/shard_map/reduce_scatter | solution.py:144
  499.6 1.6 add_convert_fusion
  (99 shorter events, 22.7 us)
Async XLA Ops:
  7.2 63.0 %all-gather.11.cloned.1.call-start = ((), (), s32[]{:S(2)}) async-start(), calls=%async_computation.2 | async-start | bytes 3244032 | tf_op jit(solution)/shard_map/all_gather | solution.py:71
  7.9 120.4 %all-gather.13.cloned.1.call-start = ((), (), s32[]{:S(2)}) async-start(), calls=%async_computation.3 | async-start | bytes 3244032 | tf_op jit(solution)/shard_map/all_gather | solution.py:72
  8.6 180.0 %all-gather.15.cloned.1.call-start = ((), (), s32[]{:S(2)}) async-start(), calls=%async_computation.4 | async-start | bytes 3244032 | tf_op jit(solution)/shard_map/all_gather | solution.py:76
  9.4 252.8 %all-gather.27.cloned.1.call-start = ((), (), s32[]{:S(2)}) async-start(), calls=%async_computation.12 | async-start | bytes 4718592 | tf_op jit(solution)/shard_map/all_gather | solution.py:100
  10.2 6.2 %copy-start.2 = (bf16[1024]{0:T(1024)(128)(2,1)S(1)}, bf16[1024]{0:T(1024)(128)(2,1)}, u32[]{:S(2)}) copy-start(bf16[1024]{0:T(1024)(128)(2,1)} %param.17) | copy-start | bytes 6148
  10.2 6.2 %copy-start = (bf16[400,1024]{1,0:T(8,128)(2,1)S(1)}, bf16[400,1024]{1,0:T(8,128)(2,1)}, u32[]{:S(2)}) copy-start(bf16[400,1024]{1,0:T(8,128)(2,1)} %param.16) | copy-start | bytes 2457604
  15.7 287.2 %all-gather.19.cloned.1.call-start = ((), (), s32[]{:S(2)}) async-start(), calls=%async_computation.7 | async-start | bytes 1179648 | tf_op jit(solution)/shard_map/all_gather | solution.py:107
  16.3 296.5 %reduce-scatter.3.cloned.1.call-start = ((), (), s32[]{:S(2)}) async-start(), calls=%async_computation.5 | async-start | bytes 2457600 | tf_op jit(solution)/shard_map/reduce_scatter | solution.py:79
  195.3 1.8 copy-start.3
  195.3 1.8 copy-start.5
  195.3 2.0 copy-start.4
  195.3 161.2 %all-gather.17.cloned.1.call-start = ((), (), s32[]{:S(2)}) async-start(), calls=%async_computation.6 | async-start | bytes 1179648 | tf_op jit(solution)/shard_map/all_gather | solution.py:105
  196.1 201.6 %all-gather.21.cloned.1.call-start = ((), (), s32[]{:S(2)}) async-start(), calls=%async_computation.8 | async-start | bytes 1179648 | tf_op jit(solution)/shard_map/all_gather | solution.py:106
  196.8 267.9 %all-gather.23.cloned.1.call-start = ((), (), s32[]{:S(2)}) async-start(), calls=%async_computation.9 | async-start | bytes 2359296 | tf_op jit(solution)/shard_map/all_gather | solution.py:14
  400.9 0.7 copy-start.1
  401.6 88.4 %all-gather.25.cloned.1.call-start = ((), (), s32[]{:S(2)}) async-start(), calls=%async_computation.10 | async-start | bytes 1179648 | tf_op jit(solution)/shard_map/all_gather | solution.py:141
  402.2 97.4 %reduce-scatter.5.cloned.1.call-start = ((), (), s32[]{:S(2)}) async-start(), calls=%async_computation.11 | async-start | bytes 393216 | tf_op jit(solution)/shard_map/reduce_scatter | solution.py:144
Sparse Core Ops, SparseCore 0:
  10.2 60.0 all-gather.10
  72.4 55.9 all-gather.12
  130.4 58.1 all-gather.14
  191.2 70.9 all-gather.26
  264.1 38.7 all-gather.18
  305.1 7.7 reduce-scatter.2
  315.0 41.5 all-gather.16
  358.7 38.9 all-gather.20
  401.7 48.3 all-gather.22
  452.0 37.9 all-gather.24
  492.8 6.7 reduce-scatter.4
